TPU v7x, 128 devices: a whole 4x4x4 slice. The times are simulated.
128 devices in a mesh: grp: 8 (over z, y_lo), dev: 16 (over x, y_hi, core).
Axes of the slice: x: 4, y: 4 (y_hi: 2, y_lo: 2; y = y_hi * 2 + y_lo), z: 4, core: 2. Of those that a mesh axis runs over, the one named last changes fastest.
Arguments:
- vertex_values: bfloat16 [8192, 128, 256], P(('grp', 'dev')), may hold values from -6 to 6
- position_domain_label: int32 [8192], P(('grp', 'dev')), may hold values from 0 to 64, as said below
- position_vertex_tally: int32 [8192], P(('grp', 'dev')), may hold values from 0 to 128, as said below
- normalizer_gain: float32 [256], replicated, may hold values from 0.1 to 1.9
- embedding_matrix: bfloat16 [256, 256], replicated, may hold values from -0.375 to 0.375
- partition_input_matrix: bfloat16 [256, 256], replicated, may hold values from -0.375 to 0.375
- partition_score_matrix: bfloat16 [32, 64], replicated, may hold values from -60 to 60
- softmax_sharpness: float32 [8], replicated, may hold values from 0.3 to 1
- partition_attention_maps: float32 [3, 32, 32], replicated, may hold values from -10 to 10
- readout_matrix: bfloat16 [256, 256], replicated, may hold values from -1.5 to 1.5
Outputs:
- updated: bfloat16 [8192, 128, 256], P(('grp', 'dev'))
Inputs may be any that keep to these rules, and one draw needn't show every extreme that they name: `position_domain_label`: on each device the used slots come first; a device may use none. Reading the devices in order and their used slots in order lists every mesh's blocks as one run, meshes in increasing order, each mesh 2 or more blocks. Exactly 4096 slots are used in all, and some device uses all 64 of its slots. `position_vertex_tally`: 128 in every used slot except the last block of each mesh, which holds 1 to 128; 0 in unused slots.
All inputs are finite; a program needn't handle non-finite values.
Results may differ from a plain program's by a relative error of at most 0.012.
The roundings to bfloat16 on the way count: a program that leaves them out, or rounds other values in their place, can miss the bound.
Values may be sent and summed in bfloat16 or wider, within the bound.
No kernel may reach another device: no remote copies, remote signals or barrier semaphores. Data moves between devices by JAX's collectives and lax.ppermute only.
A program may use at most 128 MiB of HBM per device.

v0:
```python
import jax
import jax.numpy as jnp
from jax import lax
from jax.sharding import PartitionSpec as P

MESHES = 64


def partition_routine(
    tile_sequence,
    vertex_tallies,
    domain_sequence,
    normalizer_gain,
    embedding_matrix,
    partition_input_matrix,
    partition_score_matrix,
    softmax_sharpness,
):
    tile_amount, tile_height, model_width = tile_sequence.shape
    attention_group_amount = softmax_sharpness.shape[0]
    head_width = model_width // attention_group_amount
    partition_amount = partition_score_matrix.shape[1]
    flattened = tile_sequence.reshape(tile_amount * tile_height, model_width).astype(jnp.float32)
    centre = flattened - jnp.mean(flattened, axis=1, keepdims=True)
    spread = jnp.mean(centre * centre, axis=1, keepdims=True)
    normed = (centre * lax.rsqrt(spread + 1e-05) * normalizer_gain).astype(jnp.bfloat16)
    features = jnp.dot(normed, embedding_matrix, preferred_element_type=jnp.float32).astype(
        jnp.bfloat16
    )
    middles = jnp.dot(normed, partition_input_matrix, preferred_element_type=jnp.float32).astype(
        jnp.bfloat16
    )
    partition_scores = jnp.dot(
        middles.reshape(-1, head_width), partition_score_matrix, preferred_element_type=jnp.float32
    )
    partition_scores = (
        partition_scores.reshape(tile_amount, tile_height, attention_group_amount, partition_amount)
        / softmax_sharpness[:, None]
    )
    living = (
        lax.broadcasted_iota(jnp.int32, (tile_amount, tile_height), 1) < vertex_tallies[:, None]
    ).astype(jnp.float32)
    partition_shares = (
        jax.nn.softmax(partition_scores, axis=-1) * living[:, :, None, None]
    ).astype(jnp.bfloat16)
    partial_sums = jnp.einsum(
        "bphm,bphd->bhmd",
        partition_shares,
        features.reshape(tile_amount, tile_height, attention_group_amount, head_width),
        preferred_element_type=jnp.float32,
    )
    partial_totals = jnp.sum(partition_shares.astype(jnp.float32), axis=1)
    one_hot = (
        domain_sequence[:, None] == lax.broadcasted_iota(jnp.int32, (tile_amount, MESHES), 1)
    ).astype(jnp.float32)
    domain_accumulated = jnp.dot(one_hot.T, partial_sums.reshape(tile_amount, -1))
    domain_share_accumulated = jnp.dot(one_hot.T, partial_totals.reshape(tile_amount, -1))
    return (
        partition_shares.reshape(
            tile_amount, tile_height, attention_group_amount * partition_amount
        ),
        domain_accumulated,
        domain_share_accumulated,
    )


def attend_tokens(domain_accumulated, domain_share_accumulated, partition_attention_maps):
    row_count, partition_amount = domain_share_accumulated.shape
    head_width = partition_attention_maps.shape[1]
    tokens = domain_accumulated.reshape(row_count, partition_amount, head_width) / (
        domain_share_accumulated[:, :, None] + 1.0
    )
    queries = jnp.einsum("rmd,de->rme", tokens, partition_attention_maps[0])
    key_rows = jnp.einsum("rmd,de->rme", tokens, partition_attention_maps[1])
    values = jnp.einsum("rmd,de->rme", tokens, partition_attention_maps[2])
    scores = jnp.einsum("rme,rne->rmn", queries, key_rows) * head_width ** (-0.5)
    token_probs = jax.nn.softmax(scores, axis=-1)
    blended = jnp.einsum("rmn,rne->rme", token_probs, values)
    return blended.reshape(row_count, partition_amount * head_width).astype(jnp.bfloat16)


def spread_phase(
    tile_sequence, vertex_tallies, domain_sequence, partition_shares, tokens, readout_matrix
):
    tile_amount, tile_height, model_width = tile_sequence.shape
    attention_group_amount = tokens.shape[0] // MESHES
    partition_amount = partition_shares.shape[2] // attention_group_amount
    head_width = model_width // attention_group_amount
    tables = tokens.reshape(MESHES, attention_group_amount, partition_amount, head_width)
    chosen = jnp.take(tables, jnp.minimum(domain_sequence, MESHES - 1), axis=0)
    blended = jnp.einsum(
        "bphm,bhmd->bphd",
        partition_shares.reshape(
            tile_amount, tile_height, attention_group_amount, partition_amount
        ),
        chosen,
        preferred_element_type=jnp.float32,
    ).astype(jnp.bfloat16)
    projected = jnp.dot(
        blended.reshape(-1, model_width), readout_matrix, preferred_element_type=jnp.float32
    )
    living = (
        lax.broadcasted_iota(jnp.int32, (tile_amount, tile_height), 1) < vertex_tallies[:, None]
    ).astype(jnp.float32)
    result = (
        tile_sequence.reshape(-1, model_width).astype(jnp.float32) + projected
    ) * living.reshape(-1, 1)
    return result.reshape(tile_amount, tile_height, model_width).astype(jnp.bfloat16)


def on_device(
    vertex_values,
    position_domain_label,
    position_vertex_tally,
    normalizer_gain,
    embedding_matrix,
    partition_input_matrix,
    partition_score_matrix,
    softmax_sharpness,
    partition_attention_maps,
    readout_matrix,
):
    slot_total, tile_height, model_width = vertex_values.shape
    attention_group_amount = softmax_sharpness.shape[0]
    partition_amount = partition_score_matrix.shape[1]
    group_count = slot_total // 16
    grouped = (
        vertex_values.reshape(group_count, 16, tile_height, model_width),
        position_vertex_tally.reshape(group_count, 16),
        position_domain_label.reshape(group_count, 16),
    )

    def gather_step(running, lookup_element):
        partition_shares, domain_accumulated, domain_share_accumulated = partition_routine(
            lookup_element[0],
            lookup_element[1],
            lookup_element[2],
            normalizer_gain,
            embedding_matrix,
            partition_input_matrix,
            partition_score_matrix,
            softmax_sharpness,
        )
        return (
            (running[0] + domain_accumulated, running[1] + domain_share_accumulated),
            partition_shares,
        )

    initial = (
        jnp.zeros((MESHES, model_width * partition_amount), jnp.float32),
        jnp.zeros((MESHES, attention_group_amount * partition_amount), jnp.float32),
    )
    (domain_accumulated, domain_share_accumulated), partition_shares = lax.scan(
        gather_step, initial, grouped
    )
    whole_sums, whole_totals = lax.psum(
        (
            domain_accumulated.reshape(MESHES * attention_group_amount, -1),
            domain_share_accumulated.reshape(MESHES * attention_group_amount, -1),
        ),
        ("grp", "dev"),
    )
    tokens = attend_tokens(whole_sums, whole_totals, partition_attention_maps)

    def spread_step(lookup_element):
        return spread_phase(
            lookup_element[0],
            lookup_element[1],
            lookup_element[2],
            lookup_element[3],
            tokens,
            readout_matrix,
        )

    return lax.map(spread_step, grouped + (partition_shares,)).reshape(vertex_values.shape)


def solution(mesh):
    return jax.shard_map(
        on_device,
        mesh=mesh,
        in_specs=(
            P(("grp", "dev"), None, None),
            P(("grp", "dev")),
            P(("grp", "dev")),
            P(),
            P(),
            P(),
            P(),
            P(),
            P(),
            P(),
        ),
        out_specs=P(("grp", "dev"), None, None),
        check_vma=False,
    )
```

profile of v0, /device:TPU:1, one launch (start us, length us, event | category | flops | bytes accessed | tf_op | source)
XLA Modules:
  0.0 490.3 jit_solution(10821527517631763876)
XLA Ops:
  8.0 115.3 %while.26 = (s32[]{:T(128)}, f32[64,16384]{1,0:T(8,128)}, f32[64,512]{1,0:T(8,128)S(1)}, bf16[4,16,128,512]{2,3,1,0:T(8,128)(2,1)}, s32[4,16]{1,0:T(4,128)S(1)},...) while((s32[]{:T(128)}, f32[64,16384]{1,0:T(8,128)}, ...), condition=%wide.region_6.7_spmd.clone, body=%wide.region_0.6_spmd.clone.sunk | while | flops 723058752 | bytes 48028012 | solution.py:153
  14.7 3.6 fusion.111
  27.0 3.5 reshape.222
  41.9 3.6 fusion.111
  54.2 3.5 reshape.222
  57.7 5.0 %convolution_add_fusion.5 = f32[64,16384]{1,0:T(8,128)} fusion(bf16[16,16384]{1,0:T(8,128)(2,1)S(1)} %reshape.222, f32[64,16384]{1,0:T(8,128)} %get-tuple-element.383, pred[]{:T(512)S(6)} %compare.3, s32[16]{0:T(128)S(1)} %get-tuple-element.366), kind=kOutput, calls=%fused_computation.27.clone.1 | convolution fusion | flops 35652608 | bytes 8912961 | tf_op jit(solution)/shard_map/while/body/eval_jaxpr/dot_general | solution.py:56
  71.3 3.6 fusion.111
  83.5 3.5 reshape.222
  87.0 5.0 %convolution_add_fusion.5 = f32[64,16384]{1,0:T(8,128)} fusion(bf16[16,16384]{1,0:T(8,128)(2,1)S(1)} %reshape.222, f32[64,16384]{1,0:T(8,128)} %get-tuple-element.383, pred[]{:T(512)S(6)} %compare.3, s32[16]{0:T(128)S(1)} %get-tuple-element.366), kind=kOutput, calls=%fused_computation.27.clone.1 | convolution fusion | flops 35652608 | bytes 8912961 | tf_op jit(solution)/shard_map/while/body/eval_jaxpr/dot_general | solution.py:56
  100.6 3.6 fusion.111
  112.9 3.5 reshape.222
  116.4 5.0 %convolution_add_fusion.5 = f32[64,16384]{1,0:T(8,128)} fusion(bf16[16,16384]{1,0:T(8,128)(2,1)S(1)} %reshape.222, f32[64,16384]{1,0:T(8,128)} %get-tuple-element.383, pred[]{:T(512)S(6)} %compare.3, s32[16]{0:T(128)S(1)} %get-tuple-element.366), kind=kOutput, calls=%fused_computation.27.clone.1 | convolution fusion | flops 35652608 | bytes 8912961 | tf_op jit(solution)/shard_map/while/body/eval_jaxpr/dot_general | solution.py:56
  123.3 5.0 %reshape.192 = f32[512,2048]{1,0:T(8,128)} reshape(f32[64,16384]{1,0:T(8,128)} %get-tuple-element.111) | data formatting | bytes 8388608 | tf_op jit(solution)/shard_map/reshape | solution.py:158
  129.2 157.6 %all-reduce.3.cloned.1.call-done = (f32[512,2048]{1,0:T(8,128)}, f32[512,64]{0,1:T(8,128)}) async-done(((f32[512,2048]{1,0:T(8,128)}, f32[512,64]{0,1:T(8,128)}), (f32[512,2048]{1,0:T(8,128)}, f32[512,64]{0,1:T(8,128)})) %all-reduce.3.cloned.1.call-update) | async-done | bytes 4325392 | tf_op jit(solution)/shard_map/psum | solution.py:156
  290.3 5.4 %copy.52 = f32[512,2048]{1,0:T(8,128)} copy(f32[512,2048]{0,1:T(8,128)} %bitcast.167) | data formatting | bytes 8388608 | tf_op jit(solution)/shard_map/div | solution.py:70
  295.7 5.7 %div.49 = bf16[512,2048]{1,0:T(8,128)(2,1)} divide(f32[512,2048]{1,0:T(8,128)} %get-tuple-element.218, f32[512,2048]{1,0:T(8,128)} %copy.52) | non-fusion elementwise | flops 1048576 | bytes 10485760 | tf_op jit(solution)/shard_map/div | solution.py:70
  310.6 8.8 %copy.56 = bf16[512,64,32]{1,2,0:T(8,128)(2,1)} copy(bf16[512,64,32]{0,2,1:T(8,128)(2,1)} %fusion.39) | data formatting | bytes 4194304 | tf_op jit(solution)/shard_map/rmd,de->rme/dot_general | solution.py:73
  319.3 8.9 %copy.57 = bf16[512,64,32]{1,2,0:T(8,128)(2,1)} copy(bf16[512,64,32]{0,2,1:T(8,128)(2,1)} %fusion.37) | data formatting | bytes 4194304 | tf_op jit(solution)/shard_map/rmd,de->rme/dot_general | solution.py:74
  328.3 7.9 %copy.60 = bf16[512,64,32]{1,2,0:T(8,128)(2,1)} copy(bf16[512,64,32]{0,2,1:T(8,128)(2,1)S(1)} %copy-done) | data formatting | bytes 4194304 | tf_op jit(solution)/shard_map/rmd,de->rme/dot_general | solution.py:75
  336.1 12.5 %multiply_reduce_fusion.1 = (f32[512,64]{1,0:T(8,128)S(1)}, f32[512,64,64]{1,2,0:T(8,128)}) fusion(bf16[512,64,32]{1,2,0:T(8,128)(2,1)} %copy.56, bf16[512,64,32]{1,2,0:T(8,128)(2,1)} %copy.57), kind=kOutput, calls=%fused_computation.61 | convolution fusion | flops 138379264 | bytes 12713984 | tf_op jit(solution)/shard_map/rme,rne->rmn/dot_general | solution.py:76
  348.7 10.3 %fusion.28 = f32[512,64]{1,0:T(8,128)S(1)} fusion(f32[512,64,64]{1,2,0:T(8,128)} %get-tuple-element.229, f32[512,64]{1,0:T(8,128)S(1)} %get-tuple-element.228), kind=kLoop, calls=%fused_computation.62 | loop fusion | flops 6258688 | bytes 8650752 | tf_op jit(solution)/shard_map/reduce_sum | solution.py:77
  359.0 10.4 %fusion.32 = bf16[512,64,32]{1,2,0:T(8,128)(2,1)} fusion(bf16[512,64,32]{1,2,0:T(8,128)(2,1)} %copy.60, f32[512,64,64]{1,2,0:T(8,128)} %get-tuple-element.229, f32[512,64]{1,0:T(8,128)S(1)} %fusion.28, f32[512,64]{1,0:T(8,128)S(1)} %get-tuple-element.228), kind=kOutput, calls=%fused_computation.66 | convolution fusion | flops 140509184 | bytes 12845056 | tf_op jit(solution)/shard_map/rmn,rne->rme/dot_general | solution.py:78
  369.4 6.9 %copy.61 = bf16[512,64,32]{0,2,1:T(8,128)(2,1)} copy(bf16[512,64,32]{1,2,0:T(8,128)(2,1)} %fusion.32) | data formatting | bytes 4194304 | tf_op jit(solution)/shard_map/convert_element_type | solution.py:79
  379.3 104.2 %while.25 = (s32[]{:T(128)}, bf16[4,16,128,256]{3,2,1,0:T(8,128)(2,1)}, bf16[4,16,128,256]{3,2,1,0:T(8,128)(2,1)}, s32[4,16]{1,0:T(4,128)S(1)}, bf16[512,2048]{1...) while((s32[]{:T(128)}, ...), condition=%wide.region_12.13_spmd, body=%wide.region_11.12_spmd.sunk | while | flops 338433216 | bytes 26891408 | solution.py:175
  379.6 8.0 %reshape.221 = bf16[64,8,64,32]{3,2,1,0:T(8,128)(2,1)} reshape(bf16[512,2048]{1,0:T(8,128)(2,1)S(1)} %get-tuple-element.432) | data formatting | bytes 4194304 | tf_op jit(solution)/shard_map/while/body/eval_jaxpr/reshape | solution.py:89
  387.6 8.6 %copy.92 = bf16[64,8,64,32]{2,3,1,0:T(8,128)(2,1)} copy(bf16[64,8,64,32]{3,2,1,0:T(8,128)(2,1)} %reshape.221) | data formatting | bytes 4194304 | tf_op jit(solution)/shard_map/while/body/eval_jaxpr/reshape | solution.py:89
  405.6 8.0 %reshape.221 = bf16[64,8,64,32]{3,2,1,0:T(8,128)(2,1)} reshape(bf16[512,2048]{1,0:T(8,128)(2,1)S(1)} %get-tuple-element.432) | data formatting | bytes 4194304 | tf_op jit(solution)/shard_map/while/body/eval_jaxpr/reshape | solution.py:89
  413.6 8.6 %copy.92 = bf16[64,8,64,32]{2,3,1,0:T(8,128)(2,1)} copy(bf16[64,8,64,32]{3,2,1,0:T(8,128)(2,1)} %reshape.221) | data formatting | bytes 4194304 | tf_op jit(solution)/shard_map/while/body/eval_jaxpr/reshape | solution.py:89
  431.5 8.0 %reshape.221 = bf16[64,8,64,32]{3,2,1,0:T(8,128)(2,1)} reshape(bf16[512,2048]{1,0:T(8,128)(2,1)S(1)} %get-tuple-element.432) | data formatting | bytes 4194304 | tf_op jit(solution)/shard_map/while/body/eval_jaxpr/reshape | solution.py:89
  439.6 8.6 %copy.92 = bf16[64,8,64,32]{2,3,1,0:T(8,128)(2,1)} copy(bf16[64,8,64,32]{3,2,1,0:T(8,128)(2,1)} %reshape.221) | data formatting | bytes 4194304 | tf_op jit(solution)/shard_map/while/body/eval_jaxpr/reshape | solution.py:89
  457.5 8.0 %reshape.221 = bf16[64,8,64,32]{3,2,1,0:T(8,128)(2,1)} reshape(bf16[512,2048]{1,0:T(8,128)(2,1)S(1)} %get-tuple-element.432) | data formatting | bytes 4194304 | tf_op jit(solution)/shard_map/while/body/eval_jaxpr/reshape | solution.py:89
  465.6 8.6 %copy.92 = bf16[64,8,64,32]{2,3,1,0:T(8,128)(2,1)} copy(bf16[64,8,64,32]{3,2,1,0:T(8,128)(2,1)} %reshape.221) | data formatting | bytes 4194304 | tf_op jit(solution)/shard_map/while/body/eval_jaxpr/reshape | solution.py:89
  (176 shorter events, 126.4 us)
Async XLA Ops:
  6.5 280.3 %all-reduce.3.cloned.1.call-start = ((), (), s32[]{:S(2)}) async-start(), calls=%async_computation | async-start | bytes 8650752 | tf_op jit(solution)/shard_map/psum | solution.py:156
  8.0 5.3 %copy-start.1 = (bf16[256,256]{1,0:T(8,128)(2,1)S(1)}, bf16[256,256]{1,0:T(8,128)(2,1)}, u32[]{:S(2)}) copy-start(bf16[256,256]{1,0:T(8,128)(2,1)} %get-tuple-element.403) | copy-start | bytes 393220 | tf_op jit(solution)/shard_map/while
  11.5 3.1 copy-start.5
  11.5 3.1 copy-start.6
  18.3 3.5 copy-start.2
  35.2 5.3 %copy-start.1 = (bf16[256,256]{1,0:T(8,128)(2,1)S(1)}, bf16[256,256]{1,0:T(8,128)(2,1)}, u32[]{:S(2)}) copy-start(bf16[256,256]{1,0:T(8,128)(2,1)} %get-tuple-element.403) | copy-start | bytes 393220 | tf_op jit(solution)/shard_map/while
  38.8 3.1 copy-start.5
  38.8 3.1 copy-start.6
  45.5 3.5 copy-start.2
  64.6 5.3 %copy-start.1 = (bf16[256,256]{1,0:T(8,128)(2,1)S(1)}, bf16[256,256]{1,0:T(8,128)(2,1)}, u32[]{:S(2)}) copy-start(bf16[256,256]{1,0:T(8,128)(2,1)} %get-tuple-element.403) | copy-start | bytes 393220 | tf_op jit(solution)/shard_map/while
  68.1 3.1 copy-start.5
  68.1 3.1 copy-start.6
  74.8 3.5 copy-start.2
  94.0 5.3 %copy-start.1 = (bf16[256,256]{1,0:T(8,128)(2,1)S(1)}, bf16[256,256]{1,0:T(8,128)(2,1)}, u32[]{:S(2)}) copy-start(bf16[256,256]{1,0:T(8,128)(2,1)} %get-tuple-element.403) | copy-start | bytes 393220 | tf_op jit(solution)/shard_map/while
  97.5 3.1 copy-start.5
  97.5 3.1 copy-start.6
  104.2 3.5 copy-start.2
  301.3 3.1 copy-start.3
  319.3 8.9 %copy-start = (bf16[512,64,32]{0,2,1:T(8,128)(2,1)S(1)}, bf16[512,64,32]{0,2,1:T(8,128)(2,1)}, u32[]{:S(2)}) copy-start(bf16[512,64,32]{0,2,1:T(8,128)(2,1)} %fusion.35) | copy-start | bytes 6291460
  369.4 9.9 %copy-start.4 = (bf16[256,256]{1,0:T(8,128)(2,1)S(1)}, bf16[256,256]{1,0:T(8,128)(2,1)}, u32[]{:S(2)}) copy-start(bf16[256,256]{1,0:T(8,128)(2,1)} %param.23) | copy-start | bytes 393220
Sparse Core Ops, SparseCore 0:
  129.3 157.4 all-reduce.2
where the time goes:
time: 493 us; the launch traced here: 490 us
  local copies, waits for them, and re-layouts  182 us (37%)
  waiting for transfers between devices  158 us (32%)
  matrix products  84 us (17%)
  other arithmetic  52.1 us (11%)
  between operations  13.5 us (3%)
    psum x1, waiting for transfers between devices, on_device(): lax.psum((domain_accumulated.reshape(MESHES * attention_group_amount, -1)...  158 us
    reshape x8, local copies, waits for them, and re-layouts, spread_phase(): tokens.reshape(MESHES, attention_group_amount, partition_amount, head_width)  66.4 us
    dot_general x4, matrix products, partition_routine(): jnp.dot(one_hot.T, partial_sums.reshape(tile_amount, -1))  17.9 us
    sub x4, matrix products, partition_routine(): jax.nn.softmax(partition_scores, axis=-1) * living[:, :, None, None]  14.4 us
    reshape x4, local copies, waits for them, and re-layouts, partition_routine(): partial_sums.reshape(tile_amount, -1)  14 us
    reduce_sum x4, other arithmetic, partition_routine(): partial_totals = jnp.sum(partition_shares.astype(jnp.float32), axis=1)  13.5 us
    dot_general x1, matrix products, attend_tokens(): jnp.einsum('rme,rne->rmn', queries, key_rows) * head_width ** (-0.5)  12.5 us
    gather x4, local copies, waits for them, and re-layouts, spread_phase(): chosen = jnp.take(tables, jnp.minimum(domain_sequence, MESHES - 1), axis=0)  11.7 us
  transfers between devices with their start and end apart: 1, of which 1 were waited for; matrix products, arithmetic and copies ran while one was open for 0% of the time, Pallas kernels for 0%

commit v1 on v0

--- a/solution.py
+++ b/solution.py
@@ -153,12 +153,12 @@
     (domain_accumulated, domain_share_accumulated), partition_shares = lax.scan(
         gather_step, initial, grouped
     )
-    whole_sums, whole_totals = lax.psum(
+    derive_vectors = lambda point: jax.lax.psum(jax.lax.psum(point, axis_name="grp"), "dev")
+    whole_sums, whole_totals = derive_vectors(
         (
             domain_accumulated.reshape(MESHES * attention_group_amount, -1),
             domain_share_accumulated.reshape(MESHES * attention_group_amount, -1),
-        ),
-        ("grp", "dev"),
+        )
     )
     tokens = attend_tokens(whole_sums, whole_totals, partition_attention_maps)
 

time: 493 us -> 681 us (1.38)
  waiting for transfers between devices: 158 us -> 345 us
    psum x1 -> x2, waiting for transfers between devices: 158 us -> 345 us  [the longest x1 191 us: on_device(): jax.lax.psum(point, axis_name='grp')]
  transfers between devices with their start and end apart: 1 -> 2, of which waited for: 1 -> 2; matrix products, arithmetic and copies ran while one was open for 0% -> 0% of each run, Pallas kernels for 0% -> 0%
where the time goes in v1:
time: 681 us; the launch traced here: 678 us
  waiting for transfers between devices  345 us (51%)
  local copies, waits for them, and re-layouts  182 us (27%)
  matrix products  84 us (12%)
  other arithmetic  52.1 us (8%)
  between operations  13.5 us (2%)
    psum x1, waiting for transfers between devices, on_device(): jax.lax.psum(point, axis_name='grp')  191 us
    psum x1, waiting for transfers between devices, on_device(): jax.lax.psum(jax.lax.psum(point, axis_name='grp'), 'dev')  155 us
    reshape x8, local copies, waits for them, and re-layouts, spread_phase(): tokens.reshape(MESHES, attention_group_amount, partition_amount, head_width)  66.4 us
    dot_general x4, matrix products, partition_routine(): jnp.dot(one_hot.T, partial_sums.reshape(tile_amount, -1))  17.9 us
    sub x4, matrix products, partition_routine(): jax.nn.softmax(partition_scores, axis=-1) * living[:, :, None, None]  14.4 us
    reshape x4, local copies, waits for them, and re-layouts, partition_routine(): partial_sums.reshape(tile_amount, -1)  14 us
  transfers between devices with their start and end apart: 2, of which 2 were waited for; matrix products, arithmetic and copies ran while one was open for 0% of the time, Pallas kernels for 0%

profile of v1, /device:TPU:1, one launch (start us, length us, event | category | flops | bytes accessed | tf_op | source)
XLA Modules:
  0.0 678.0 jit_solution(13464356286495240531)
XLA Ops:
  8.0 115.3 %while.26 = (s32[]{:T(128)}, f32[64,16384]{1,0:T(8,128)}, f32[64,512]{1,0:T(8,128)S(1)}, bf16[4,16,128,512]{2,3,1,0:T(8,128)(2,1)}, s32[4,16]{1,0:T(4,128)S(1)},...) while((s32[]{:T(128)}, f32[64,16384]{1,0:T(8,128)}, ...), condition=%wide.region_6.7_spmd.clone, body=%wide.region_0.6_spmd.clone.sunk | while | flops 723058752 | bytes 48028012 | solution.py:153
  14.7 3.6 fusion.111
  27.0 3.5 reshape.222
  41.9 3.6 fusion.111
  54.2 3.5 reshape.222
  57.7 5.0 convolution_add_fusion.5
  71.3 3.6 fusion.111
  83.5 3.5 reshape.222
  87.0 5.0 convolution_add_fusion.5
  100.6 3.6 fusion.111
  116.4 5.0 convolution_add_fusion.5
  123.3 4.9 reshape.192
  129.4 190.6 %all-reduce.7.cloned.1.call-done = (f32[512,2048]{1,0:T(8,128)}, f32[512,64]{0,1:T(8,128)}) async-done(((f32[512,2048]{1,0:T(8,128)}, f32[512,64]{0,1:T(8,128)}), (f32[512,2048]{1,0:T(8,128)}, f32[512,64]{0,1:T(8,128)})) %all-reduce.7.cloned.1.call-update) | async-done | bytes 4325392 | tf_op jit(solution)/shard_map/psum | solution.py:156
  320.1 154.7 %all-reduce.5.cloned.1.call-done = (f32[512,2048]{1,0:T(8,128)}, f32[512,64]{0,1:T(8,128)}) async-done(((f32[512,2048]{1,0:T(8,128)}, f32[512,64]{0,1:T(8,128)}), (f32[512,2048]{1,0:T(8,128)}, f32[512,64]{0,1:T(8,128)})) %all-reduce.5.cloned.1.call-update) | async-done | bytes 4325392 | tf_op jit(solution)/shard_map/psum | solution.py:156
  478.2 5.4 copy.52
  483.6 5.7 div.49
  498.3 8.8 %copy.56 = bf16[512,64,32]{1,2,0:T(8,128)(2,1)} copy(bf16[512,64,32]{0,2,1:T(8,128)(2,1)} %fusion.39) | data formatting | bytes 4194304 | tf_op jit(solution)/shard_map/rmd,de->rme/dot_general | solution.py:73
  507.1 8.9 %copy.57 = bf16[512,64,32]{1,2,0:T(8,128)(2,1)} copy(bf16[512,64,32]{0,2,1:T(8,128)(2,1)} %fusion.37) | data formatting | bytes 4194304 | tf_op jit(solution)/shard_map/rmd,de->rme/dot_general | solution.py:74
  516.0 7.9 %copy.60 = bf16[512,64,32]{1,2,0:T(8,128)(2,1)} copy(bf16[512,64,32]{0,2,1:T(8,128)(2,1)S(1)} %copy-done) | data formatting | bytes 4194304 | tf_op jit(solution)/shard_map/rmd,de->rme/dot_general | solution.py:75
  523.9 12.5 %multiply_reduce_fusion.1 = (f32[512,64]{1,0:T(8,128)S(1)}, f32[512,64,64]{1,2,0:T(8,128)}) fusion(bf16[512,64,32]{1,2,0:T(8,128)(2,1)} %copy.56, bf16[512,64,32]{1,2,0:T(8,128)(2,1)} %copy.57), kind=kOutput, calls=%fused_computation.61 | convolution fusion | flops 138379264 | bytes 12713984 | tf_op jit(solution)/shard_map/rme,rne->rmn/dot_general | solution.py:76
  536.4 10.3 %fusion.28 = f32[512,64]{1,0:T(8,128)S(1)} fusion(f32[512,64,64]{1,2,0:T(8,128)} %get-tuple-element.231, f32[512,64]{1,0:T(8,128)S(1)} %get-tuple-element.230), kind=kLoop, calls=%fused_computation.62 | loop fusion | flops 6258688 | bytes 8650752 | tf_op jit(solution)/shard_map/reduce_sum | solution.py:77
  546.7 10.4 %fusion.32 = bf16[512,64,32]{1,2,0:T(8,128)(2,1)} fusion(bf16[512,64,32]{1,2,0:T(8,128)(2,1)} %copy.60, f32[512,64,64]{1,2,0:T(8,128)} %get-tuple-element.231, f32[512,64]{1,0:T(8,128)S(1)} %fusion.28, f32[512,64]{1,0:T(8,128)S(1)} %get-tuple-element.230), kind=kOutput, calls=%fused_computation.66 | convolution fusion | flops 140509184 | bytes 12845056 | tf_op jit(solution)/shard_map/rmn,rne->rme/dot_general | solution.py:78
  557.1 6.9 %copy.61 = bf16[512,64,32]{0,2,1:T(8,128)(2,1)} copy(bf16[512,64,32]{1,2,0:T(8,128)(2,1)} %fusion.32) | data formatting | bytes 4194304 | tf_op jit(solution)/shard_map/convert_element_type | solution.py:79
  567.0 104.2 %while.25 = (s32[]{:T(128)}, bf16[4,16,128,256]{3,2,1,0:T(8,128)(2,1)}, bf16[4,16,128,256]{3,2,1,0:T(8,128)(2,1)}, s32[4,16]{1,0:T(4,128)S(1)}, bf16[512,2048]{1...) while((s32[]{:T(128)}, ...), condition=%wide.region_14.15_spmd, body=%wide.region_13.14_spmd.sunk | while | flops 338433216 | bytes 26891408 | solution.py:175
  567.3 8.0 %reshape.221 = bf16[64,8,64,32]{3,2,1,0:T(8,128)(2,1)} reshape(bf16[512,2048]{1,0:T(8,128)(2,1)S(1)} %get-tuple-element.434) | data formatting | bytes 4194304 | tf_op jit(solution)/shard_map/while/body/eval_jaxpr/reshape | solution.py:89
  575.3 8.6 %copy.92 = bf16[64,8,64,32]{2,3,1,0:T(8,128)(2,1)} copy(bf16[64,8,64,32]{3,2,1,0:T(8,128)(2,1)} %reshape.221) | data formatting | bytes 4194304 | tf_op jit(solution)/shard_map/while/body/eval_jaxpr/reshape | solution.py:89
  593.3 8.0 %reshape.221 = bf16[64,8,64,32]{3,2,1,0:T(8,128)(2,1)} reshape(bf16[512,2048]{1,0:T(8,128)(2,1)S(1)} %get-tuple-element.434) | data formatting | bytes 4194304 | tf_op jit(solution)/shard_map/while/body/eval_jaxpr/reshape | solution.py:89
  601.3 8.6 %copy.92 = bf16[64,8,64,32]{2,3,1,0:T(8,128)(2,1)} copy(bf16[64,8,64,32]{3,2,1,0:T(8,128)(2,1)} %reshape.221) | data formatting | bytes 4194304 | tf_op jit(solution)/shard_map/while/body/eval_jaxpr/reshape | solution.py:89
  619.3 8.0 %reshape.221 = bf16[64,8,64,32]{3,2,1,0:T(8,128)(2,1)} reshape(bf16[512,2048]{1,0:T(8,128)(2,1)S(1)} %get-tuple-element.434) | data formatting | bytes 4194304 | tf_op jit(solution)/shard_map/while/body/eval_jaxpr/reshape | solution.py:89
  627.3 8.6 %copy.92 = bf16[64,8,64,32]{2,3,1,0:T(8,128)(2,1)} copy(bf16[64,8,64,32]{3,2,1,0:T(8,128)(2,1)} %reshape.221) | data formatting | bytes 4194304 | tf_op jit(solution)/shard_map/while/body/eval_jaxpr/reshape | solution.py:89
  645.2 8.0 %reshape.221 = bf16[64,8,64,32]{3,2,1,0:T(8,128)(2,1)} reshape(bf16[512,2048]{1,0:T(8,128)(2,1)S(1)} %get-tuple-element.434) | data formatting | bytes 4194304 | tf_op jit(solution)/shard_map/while/body/eval_jaxpr/reshape | solution.py:89
  653.3 8.6 %copy.92 = bf16[64,8,64,32]{2,3,1,0:T(8,128)(2,1)} copy(bf16[64,8,64,32]{3,2,1,0:T(8,128)(2,1)} %reshape.221) | data formatting | bytes 4194304 | tf_op jit(solution)/shard_map/while/body/eval_jaxpr/reshape | solution.py:89
  (179 shorter events, 129.9 us)
Async XLA Ops:
  6.5 313.5 %all-reduce.7.cloned.1.call-start = ((), (), s32[]{:S(2)}) async-start(), calls=%async_computation.1 | async-start | bytes 8650752 | tf_op jit(solution)/shard_map/psum | solution.py:156
  8.0 5.3 copy-start.1
  11.5 3.1 copy-start.5
  11.5 3.1 copy-start.6
  18.3 3.5 copy-start.2
  35.2 5.3 copy-start.1
  38.8 3.1 copy-start.5
  38.8 3.1 copy-start.6
  45.5 3.5 copy-start.2
  64.6 5.3 copy-start.1
  68.1 3.1 copy-start.5
  68.1 3.1 copy-start.6
  74.8 3.5 copy-start.2
  93.9 5.3 copy-start.1
  97.5 3.1 copy-start.5
  97.5 3.1 copy-start.6
  104.2 3.5 copy-start.2
  129.2 345.6 %all-reduce.5.cloned.1.call-start = ((), (), s32[]{:S(2)}) async-start(), calls=%async_computation | async-start | bytes 8650752 | tf_op jit(solution)/shard_map/psum | solution.py:156
  489.2 2.9 copy-start.3
  507.1 8.9 %copy-start = (bf16[512,64,32]{0,2,1:T(8,128)(2,1)S(1)}, bf16[512,64,32]{0,2,1:T(8,128)(2,1)}, u32[]{:S(2)}) copy-start(bf16[512,64,32]{0,2,1:T(8,128)(2,1)} %fusion.35) | copy-start | bytes 6291460
  557.1 9.9 %copy-start.4 = (bf16[256,256]{1,0:T(8,128)(2,1)S(1)}, bf16[256,256]{1,0:T(8,128)(2,1)}, u32[]{:S(2)}) copy-start(bf16[256,256]{1,0:T(8,128)(2,1)} %param.23) | copy-start | bytes 393220
Sparse Core Ops, SparseCore 0:
  129.3 190.6 all-reduce.6
  322.6 152.0 all-reduce.4
